TPU v7x, 32 devices: a whole 2x2x4 slice. The times are simulated.
32 devices in a mesh: gene: 8 (over z, x), cell: 4 (over y, core).
Axes of the slice: x: 2, y: 2, z: 4, core: 2. Of those that a mesh axis runs over, the one named last changes fastest.
Arguments:
- pool_counts: bfloat16 [20480, 16384], P('gene', 'cell'), may hold values from 0 to 6.5
- cell_picks: int32 [7, 4096], P(None, 'cell'), may hold values from 0 to 16383, as said below
- loadings_init: float32 [64, 20480], P(None, 'gene'), may hold values from -0.0390625 to 0.0390625
Outputs:
- scaled_loadings: float32 [64, 20480], P(None, 'gene')
Inputs may be any that keep to these rules, and one draw needn't show every extreme that they name: `cell_picks`: column b of every row names a pool cell in [(b // 1024) * 4096, (b // 1024 + 1) * 4096); no cell is named twice in one row.
All inputs are finite; a program needn't handle non-finite values.
Results may differ from a plain program's by a relative error of at most 0.018.
Values may be sent and summed in bfloat16 or wider, within the bound.
A program may use at most 128 MiB of HBM per device.

v0:
```python
import math
import jax
import jax.numpy as jnp
from jax import lax
from jax.sharding import PartitionSpec as P

STEPS = 7
step_rate = 1.0


def transposed_product(left, right):
    return lax.dot_general(
        left, right, (((1,), (1,)), ((), ())), preferred_element_type=jnp.float32
    )


def shards(pool_counts, cell_picks, loadings_init):
    loadings = loadings_init
    local_pool = pool_counts.shape[1]
    group = lax.axis_index("cell")
    batch_total = cell_picks.shape[1] * lax.axis_size("cell")
    gene_total = loadings.shape[1] * lax.axis_size("gene")
    for step_index in range(STEPS):
        chosen = cell_picks[step_index] - group * local_pool
        gathered = jnp.take(pool_counts, chosen, axis=1)
        weights_low = loadings.astype(jnp.bfloat16)
        product = jnp.dot(weights_low, gathered, preferred_element_type=jnp.float32)
        local_sums = jnp.sum(gathered, axis=1, dtype=jnp.float32)
        batch_means = lax.psum(local_sums, "cell") / batch_total
        shift = jnp.dot(
            weights_low.astype(jnp.float32), batch_means, precision=lax.Precision.HIGHEST
        )
        partial_value = product - shift[:, None]
        scores = lax.psum(partial_value, "gene")
        scores_low = scores.astype(jnp.bfloat16)
        raw_update = transposed_product(scores_low, gathered)
        row_totals = jnp.sum(scores_low, axis=1, dtype=jnp.float32)
        local_update = (raw_update - row_totals[:, None] * batch_means[None, :]) / batch_total
        update = lax.psum(local_update.astype(jnp.bfloat16), "cell").astype(jnp.float32)
        stepped = loadings + step_rate * update
        gram_part = jnp.dot(stepped, stepped.T, precision=lax.Precision.HIGHEST)
        gram_matrix = lax.psum(gram_part, "gene")
        factor = jnp.linalg.cholesky(gram_matrix)
        loadings = lax.linalg.triangular_solve(factor, stepped, left_side=True, lower=True)
    return loadings * math.sqrt(gene_total)


def solution(mesh):
    placed = (P("gene", "cell"), P(None, "cell"), P(None, "gene"))
    return jax.shard_map(
        shards, mesh=mesh, in_specs=placed, out_specs=P(None, "gene"), check_vma=False
    )
```

profile of v0, /device:TPU:0, one launch (start us, length us, event | category | flops | bytes accessed | tf_op | source)
XLA Modules:
  0.0 1143.4 jit_solution(7488319310404820462)
XLA Ops:
  7.8 25.9 %copy.4 = bf16[2560,4096]{0,1:T(8,128)(2,1)} copy(bf16[2560,4096]{1,0:T(8,128)(2,1)} %param.8) | data formatting | bytes 41943040 | tf_op args[0]
  73.9 20.5 %gather_fusion.4 = bf16[1024,2560]{1,0:T(8,128)(2,1)} fusion(bf16[2560,4096]{0,1:T(8,128)(2,1)} %copy.4, s32[1024]{0:T(1024)S(1)} %fusion.186), kind=kCustom, calls=%fused_computation.4.clone | custom fusion | bytes 10489856 | tf_op jit(solution)/shard_map/jit(_take)/gather | solution.py:25
  195.6 33.5 %all-reduce.31.cloned.1.call-done = (f32[2560]{0:T(1024)}, f32[2560]{0:T(1024)}, f32[2560]{0:T(1024)}, f32[2560]{0:T(1024)}, f32[2560]{0:T(1024)}, /*index=5*/f32[2560]{0:T(1024)}, f32[2560]{0:T(1024)}) async-done(((f32[2560]{0:T(1024)}, f32[2560]{0:T(1024)}, f32[2560]{0:T(1024)}, f32[2560]{0:T(1024)}, f32[2560]{0:T(1024)}, /*index=5*/f32[2560]{0:T(1024)}, f32[2560]{0:T(1024)}), (f32[2560]{0:T(1024)}, ...) | async-done | bytes 71696 | tf_op jit(solution)/shard_map/psum | solution.py:29
  234.5 40.8 %all-reduce.32 = bf16[64,1024]{1,0:T(8,128)(2,1)S(1)} all-reduce(f32[64,1024]{1,0:T(8,128)S(1)} %fusion.94), channel_id=1, replica_groups=mesh['gene'=8,'cell'=4] {'gene'}, use_global_device_ids=true, to_apply=%region_2.4 | all-reduce | flops 65536 | bytes 393216 | tf_op jit(solution)/shard_map/psum | solution.py:34
  279.9 30.0 %all-reduce.17.cloned.1.call-done = bf16[64,2560]{1,0:T(8,128)(2,1)} async-done(((bf16[64,2560]{1,0:T(8,128)(2,1)}), bf16[64,2560]{1,0:T(8,128)(2,1)}) %all-reduce.17.cloned.1.call-update) | async-done | bytes 327696 | tf_op jit(solution)/shard_map/psum | solution.py:39
  311.8 37.1 %psum.199 = f32[64,64]{0,1:T(8,128)S(1)} all-reduce(f32[64,64]{0,1:T(8,128)S(1)} %fusion.116), channel_id=1, replica_groups=mesh['gene'=8,'cell'=4] {'gene'}, use_global_device_ids=true, to_apply=%region_5.7 | all-reduce | flops 4096 | bytes 32768 | tf_op jit(solution)/shard_map/psum | solution.py:42
  367.4 36.0 %all-reduce.33 = bf16[64,1024]{1,0:T(8,128)(2,1)S(1)} all-reduce(f32[64,1024]{1,0:T(8,128)S(1)} %fusion.97), channel_id=1, replica_groups=mesh['gene'=8,'cell'=4] {'gene'}, use_global_device_ids=true, to_apply=%region_10.0 | all-reduce | flops 65536 | bytes 393216 | tf_op jit(solution)/shard_map/psum | solution.py:34
  408.1 30.5 %all-reduce.19.cloned.1.call-done = bf16[64,2560]{1,0:T(8,128)(2,1)} async-done(((bf16[64,2560]{1,0:T(8,128)(2,1)}), bf16[64,2560]{1,0:T(8,128)(2,1)}) %all-reduce.19.cloned.1.call-update) | async-done | bytes 327696 | tf_op jit(solution)/shard_map/psum | solution.py:39
  440.4 37.6 %psum.203 = f32[64,64]{0,1:T(8,128)S(1)} all-reduce(f32[64,64]{0,1:T(8,128)S(1)} %fusion.118), channel_id=1, replica_groups=mesh['gene'=8,'cell'=4] {'gene'}, use_global_device_ids=true, to_apply=%region_13.0 | all-reduce | flops 4096 | bytes 32768 | tf_op jit(solution)/shard_map/psum | solution.py:42
  496.6 36.0 %all-reduce.34 = bf16[64,1024]{1,0:T(8,128)(2,1)S(1)} all-reduce(f32[64,1024]{1,0:T(8,128)S(1)} %fusion.100), channel_id=1, replica_groups=mesh['gene'=8,'cell'=4] {'gene'}, use_global_device_ids=true, to_apply=%region_16.0 | all-reduce | flops 65536 | bytes 393216 | tf_op jit(solution)/shard_map/psum | solution.py:34
  537.2 30.6 %all-reduce.21.cloned.1.call-done = bf16[64,2560]{1,0:T(8,128)(2,1)} async-done(((bf16[64,2560]{1,0:T(8,128)(2,1)}), bf16[64,2560]{1,0:T(8,128)(2,1)}) %all-reduce.21.cloned.1.call-update) | async-done | bytes 327696 | tf_op jit(solution)/shard_map/psum | solution.py:39
  569.7 37.1 %psum.207 = f32[64,64]{0,1:T(8,128)S(1)} all-reduce(f32[64,64]{0,1:T(8,128)S(1)} %fusion.120), channel_id=1, replica_groups=mesh['gene'=8,'cell'=4] {'gene'}, use_global_device_ids=true, to_apply=%region_19.0 | all-reduce | flops 4096 | bytes 32768 | tf_op jit(solution)/shard_map/psum | solution.py:42
  625.3 36.0 %all-reduce.35 = bf16[64,1024]{1,0:T(8,128)(2,1)S(1)} all-reduce(f32[64,1024]{1,0:T(8,128)S(1)} %fusion.103), channel_id=1, replica_groups=mesh['gene'=8,'cell'=4] {'gene'}, use_global_device_ids=true, to_apply=%region_22.0 | all-reduce | flops 65536 | bytes 393216 | tf_op jit(solution)/shard_map/psum | solution.py:34
  666.2 30.4 %all-reduce.23.cloned.1.call-done = bf16[64,2560]{1,0:T(8,128)(2,1)} async-done(((bf16[64,2560]{1,0:T(8,128)(2,1)}), bf16[64,2560]{1,0:T(8,128)(2,1)}) %all-reduce.23.cloned.1.call-update) | async-done | bytes 327696 | tf_op jit(solution)/shard_map/psum | solution.py:39
  698.4 37.1 %psum.211 = f32[64,64]{0,1:T(8,128)S(1)} all-reduce(f32[64,64]{0,1:T(8,128)S(1)} %fusion.122), channel_id=1, replica_groups=mesh['gene'=8,'cell'=4] {'gene'}, use_global_device_ids=true, to_apply=%region_25.0 | all-reduce | flops 4096 | bytes 32768 | tf_op jit(solution)/shard_map/psum | solution.py:42
  754.0 36.0 %all-reduce.36 = bf16[64,1024]{1,0:T(8,128)(2,1)S(1)} all-reduce(f32[64,1024]{1,0:T(8,128)S(1)} %fusion.106), channel_id=1, replica_groups=mesh['gene'=8,'cell'=4] {'gene'}, use_global_device_ids=true, to_apply=%region_28.0 | all-reduce | flops 65536 | bytes 393216 | tf_op jit(solution)/shard_map/psum | solution.py:34
  794.6 30.7 %all-reduce.25.cloned.1.call-done = bf16[64,2560]{1,0:T(8,128)(2,1)} async-done(((bf16[64,2560]{1,0:T(8,128)(2,1)}), bf16[64,2560]{1,0:T(8,128)(2,1)}) %all-reduce.25.cloned.1.call-update) | async-done | bytes 327696 | tf_op jit(solution)/shard_map/psum | solution.py:39
  827.1 37.1 %psum.215 = f32[64,64]{0,1:T(8,128)S(1)} all-reduce(f32[64,64]{0,1:T(8,128)S(1)} %fusion.124), channel_id=1, replica_groups=mesh['gene'=8,'cell'=4] {'gene'}, use_global_device_ids=true, to_apply=%region_31.0 | all-reduce | flops 4096 | bytes 32768 | tf_op jit(solution)/shard_map/psum | solution.py:42
  882.8 36.2 %all-reduce.37 = bf16[64,1024]{1,0:T(8,128)(2,1)S(1)} all-reduce(f32[64,1024]{1,0:T(8,128)S(1)} %fusion.109), channel_id=1, replica_groups=mesh['gene'=8,'cell'=4] {'gene'}, use_global_device_ids=true, to_apply=%region_34.0 | all-reduce | flops 65536 | bytes 393216 | tf_op jit(solution)/shard_map/psum | solution.py:34
  923.6 30.5 %all-reduce.27.cloned.1.call-done = bf16[64,2560]{1,0:T(8,128)(2,1)} async-done(((bf16[64,2560]{1,0:T(8,128)(2,1)}), bf16[64,2560]{1,0:T(8,128)(2,1)}) %all-reduce.27.cloned.1.call-update) | async-done | bytes 327696 | tf_op jit(solution)/shard_map/psum | solution.py:39
  956.0 37.1 %psum.219 = f32[64,64]{0,1:T(8,128)S(1)} all-reduce(f32[64,64]{0,1:T(8,128)S(1)} %fusion.126), channel_id=1, replica_groups=mesh['gene'=8,'cell'=4] {'gene'}, use_global_device_ids=true, to_apply=%region_37.0 | all-reduce | flops 4096 | bytes 32768 | tf_op jit(solution)/shard_map/psum | solution.py:42
  1011.6 35.9 %all-reduce.38 = bf16[64,1024]{1,0:T(8,128)(2,1)S(1)} all-reduce(f32[64,1024]{1,0:T(8,128)S(1)} %fusion.112), channel_id=1, replica_groups=mesh['gene'=8,'cell'=4] {'gene'}, use_global_device_ids=true, to_apply=%region_40.0 | all-reduce | flops 65536 | bytes 393216 | tf_op jit(solution)/shard_map/psum | solution.py:34
  1052.1 30.7 %all-reduce.29.cloned.1.call-done = bf16[64,2560]{1,0:T(8,128)(2,1)} async-done(((bf16[64,2560]{1,0:T(8,128)(2,1)}), bf16[64,2560]{1,0:T(8,128)(2,1)}) %all-reduce.29.cloned.1.call-update) | async-done | bytes 327696 | tf_op jit(solution)/shard_map/psum | solution.py:39
  1084.5 37.1 %psum.223 = f32[64,64]{0,1:T(8,128)S(1)} all-reduce(f32[64,64]{0,1:T(8,128)S(1)} %fusion.127), channel_id=1, replica_groups=mesh['gene'=8,'cell'=4] {'gene'}, use_global_device_ids=true, to_apply=%region_43.47 | all-reduce | flops 4096 | bytes 32768 | tf_op jit(solution)/shard_map/psum | solution.py:42
  (175 shorter events, 318.5 us)
Async XLA Ops:
  6.5 222.6 %all-reduce.31.cloned.1.call-start = ((), (), s32[]{:S(2)}) async-start(), calls=%async_computation.7 | async-start | bytes 172032 | tf_op jit(solution)/shard_map/psum | solution.py:29
  175.0 11.6 %slice-start = ((s8[5242880]{0:T(1024)(128)(4,1)}), s8[1048576]{0:T(1024)(128)(4,1)S(1)}, s32[]{:S(2)}) async-start(s8[5242880]{0:T(1024)(128)(4,1)} %bitcast.200), calls=%async_computation.8 | async-start | bytes 2097152
  179.3 7.3 slice-start.1
  179.3 12.7 %slice-start.2 = ((s8[5242880]{0:T(1024)(128)(4,1)}), s8[4194304]{0:T(1024)(128)(4,1)S(1)}, s32[]{:S(2)}) async-start(s8[5242880]{0:T(1024)(128)(4,1)} %bitcast.202), calls=%async_computation.10 | async-start | bytes 8388608
  179.3 12.7 %slice-start.4 = ((s8[5242880]{0:T(1024)(128)(4,1)}), s8[4194304]{0:T(1024)(128)(4,1)S(1)}, s32[]{:S(2)}) async-start(s8[5242880]{0:T(1024)(128)(4,1)} %bitcast.204), calls=%async_computation.12 | async-start | bytes 8388608
  186.6 5.4 slice-start.3
  186.6 5.4 slice-start.5
  192.0 37.8 %copy-start = (f32[64,2560]{1,0:T(8,128)S(1)}, f32[64,2560]{1,0:T(8,128)}, u32[]{:S(2)}) copy-start(f32[64,2560]{1,0:T(8,128)} %param.10) | copy-start | bytes 1966084
  195.6 114.4 %all-reduce.17.cloned.1.call-start = ((), (), s32[]{:S(2)}) async-start(), calls=%async_computation | async-start | bytes 655360 | tf_op jit(solution)/shard_map/psum | solution.py:39
  234.5 45.4 %copy-start.6 = (f32[2560]{0:T(1024)S(1)}, f32[2560]{0:T(1024)}, u32[]{:S(2)}) copy-start(f32[2560]{0:T(1024)} %get-tuple-element.8) | copy-start | bytes 30724
  279.8 158.7 %all-reduce.19.cloned.1.call-start = ((), (), s32[]{:S(2)}) async-start(), calls=%async_computation.1 | async-start | bytes 655360 | tf_op jit(solution)/shard_map/psum | solution.py:39
  367.4 40.6 %copy-start.5 = (f32[2560]{0:T(1024)S(1)}, f32[2560]{0:T(1024)}, u32[]{:S(2)}) copy-start(f32[2560]{0:T(1024)} %get-tuple-element.10) | copy-start | bytes 30724
  408.0 159.9 %all-reduce.21.cloned.1.call-start = ((), (), s32[]{:S(2)}) async-start(), calls=%async_computation.2 | async-start | bytes 655360 | tf_op jit(solution)/shard_map/psum | solution.py:39
  496.6 40.6 %copy-start.4 = (f32[2560]{0:T(1024)S(1)}, f32[2560]{0:T(1024)}, u32[]{:S(2)}) copy-start(f32[2560]{0:T(1024)} %get-tuple-element.11) | copy-start | bytes 30724
  537.1 159.4 %all-reduce.23.cloned.1.call-start = ((), (), s32[]{:S(2)}) async-start(), calls=%async_computation.3 | async-start | bytes 655360 | tf_op jit(solution)/shard_map/psum | solution.py:39
  625.3 40.8 %copy-start.3 = (f32[2560]{0:T(1024)S(1)}, f32[2560]{0:T(1024)}, u32[]{:S(2)}) copy-start(f32[2560]{0:T(1024)} %get-tuple-element.12) | copy-start | bytes 30724
  665.9 159.4 %all-reduce.25.cloned.1.call-start = ((), (), s32[]{:S(2)}) async-start(), calls=%async_computation.4 | async-start | bytes 655360 | tf_op jit(solution)/shard_map/psum | solution.py:39
  754.0 40.6 %copy-start.2 = (f32[2560]{0:T(1024)S(1)}, f32[2560]{0:T(1024)}, u32[]{:S(2)}) copy-start(f32[2560]{0:T(1024)} %get-tuple-element.13) | copy-start | bytes 30724
  794.5 159.6 %all-reduce.27.cloned.1.call-start = ((), (), s32[]{:S(2)}) async-start(), calls=%async_computation.5 | async-start | bytes 655360 | tf_op jit(solution)/shard_map/psum | solution.py:39
  882.8 40.9 %copy-start.1 = (f32[2560]{0:T(1024)S(1)}, f32[2560]{0:T(1024)}, u32[]{:S(2)}) copy-start(f32[2560]{0:T(1024)} %get-tuple-element.14) | copy-start | bytes 30724
  923.5 159.2 %all-reduce.29.cloned.1.call-start = ((), (), s32[]{:S(2)}) async-start(), calls=%async_computation.6 | async-start | bytes 655360 | tf_op jit(solution)/shard_map/psum | solution.py:39
Sparse Core Ops, SparseCore 0:
  195.7 33.3 all-reduce.30
  280.0 29.9 all-reduce.16
  408.1 30.4 all-reduce.18
  537.3 30.5 all-reduce.20
  666.0 30.5 all-reduce.22
  794.7 30.5 all-reduce.24
  923.7 30.4 all-reduce.26
  1052.2 30.4 all-reduce.28
where the time goes:
time: 1150 us; the launch traced here: 1140 us
  blocking collectives  517 us (45%)
  waiting for transfers between devices  247 us (21%)
  local copies, waits for them, and re-layouts  168 us (15%)
  other arithmetic  108 us (9%)
  matrix products  88.8 us (8%)
  between operations  14.4 us (1%)
    psum x7, blocking collectives, shards(): gram_matrix = lax.psum(gram_part, 'gene')  260 us
    psum x7, blocking collectives, shards(): scores = lax.psum(partial_value, 'gene')  257 us
    psum x7, waiting for transfers between devices, shards(): lax.psum(local_update.astype(jnp.bfloat16), 'cell').astype(jnp.float32)  213 us
    gather x7, local copies, waits for them, and re-layouts, shards(): gathered = jnp.take(pool_counts, chosen, axis=1)  141 us
    another operation x21, other arithmetic, shards(): factor = jnp.linalg.cholesky(gram_matrix)  45.6 us
    another operation x14, other arithmetic, shards(): lax.linalg.triangular_solve(factor, stepped, left_side=True, lower=True)  38.8 us
    psum x1, waiting for transfers between devices, shards(): batch_means = lax.psum(local_sums, 'cell') / batch_total  33.5 us
    dot_general x7, matrix products, transposed_product(): lax.dot_general(left, right, (((1,), (1,)), ((), ())), preferred_element_...  30.7 us
  transfers between devices with their start and end apart: 8, of which 8 were waited for; matrix products, arithmetic and copies ran while one was open for 0% of the time, Pallas kernels for 0%

commit v1 on v0

--- a/solution.py
+++ b/solution.py
@@ -39,7 +39,7 @@
         update = lax.psum(local_update.astype(jnp.bfloat16), "cell").astype(jnp.float32)
         stepped = loadings + step_rate * update
         gram_part = jnp.dot(stepped, stepped.T, precision=lax.Precision.HIGHEST)
-        gram_matrix = lax.psum(gram_part, "gene")
+        gram_matrix = jnp.sum(lax.all_gather(gram_part, "gene"), axis=0)
         factor = jnp.linalg.cholesky(gram_matrix)
         loadings = lax.linalg.triangular_solve(factor, stepped, left_side=True, lower=True)
     return loadings * math.sqrt(gene_total)

time: 1150 us -> 1130 us (0.983)
  blocking collectives: 517 us -> 498 us
    psum x7 -> x0, blocking collectives: 260 us -> none  [shards(): gram_matrix = lax.psum(gram_part, 'gene')]
    all_gather x0 -> x7, blocking collectives: none -> 217 us  [shards(): gram_matrix = jnp.sum(lax.all_gather(gram_part, 'gene'), axis=0)]
    psum x7, blocking collectives: 257 us -> 281 us  [shards(): scores = lax.psum(partial_value, 'gene')]
where the time goes in v1:
time: 1130 us; the launch traced here: 1120 us
  blocking collectives  498 us (44%)
  waiting for transfers between devices  237 us (21%)
  local copies, waits for them, and re-layouts  168 us (15%)
  other arithmetic  108 us (10%)
  matrix products  88.8 us (8%)
  between operations  14.4 us (1%)
    psum x7, blocking collectives, shards(): scores = lax.psum(partial_value, 'gene')  281 us
    all_gather x7, blocking collectives, shards(): gram_matrix = jnp.sum(lax.all_gather(gram_part, 'gene'), axis=0)  217 us
    psum x7, waiting for transfers between devices, shards(): lax.psum(local_update.astype(jnp.bfloat16), 'cell').astype(jnp.float32)  204 us
    gather x7, local copies, waits for them, and re-layouts, shards(): gathered = jnp.take(pool_counts, chosen, axis=1)  141 us
    another operation x21, other arithmetic, shards(): factor = jnp.linalg.cholesky(gram_matrix)  45.6 us
    another operation x14, other arithmetic, shards(): lax.linalg.triangular_solve(factor, stepped, left_side=True, lower=True)  38.8 us
    psum x1, waiting for transfers between devices, shards(): batch_means = lax.psum(local_sums, 'cell') / batch_total  33.5 us
    dot_general x7, matrix products, transposed_product(): lax.dot_general(left, right, (((1,), (1,)), ((), ())), preferred_element_...  30.8 us
  transfers between devices with their start and end apart: 8, of which 8 were waited for; matrix products, arithmetic and copies ran while one was open for 0% of the time, Pallas kernels for 0%

profile of v1, /device:TPU:0, one launch (start us, length us, event | category | flops | bytes accessed | tf_op | source)
XLA Modules:
  0.0 1115.2 jit_solution(12930984549426212991)
XLA Ops:
  7.8 25.9 %copy.18 = bf16[2560,4096]{0,1:T(8,128)(2,1)} copy(bf16[2560,4096]{1,0:T(8,128)(2,1)} %param.8) | data formatting | bytes 41943040 | tf_op args[0]
  73.9 20.5 %gather_fusion.4 = bf16[1024,2560]{1,0:T(8,128)(2,1)} fusion(bf16[2560,4096]{0,1:T(8,128)(2,1)} %copy.18, s32[1024]{0:T(1024)S(1)} %fusion.186), kind=kCustom, calls=%fused_computation.4.clone | custom fusion | bytes 10489856 | tf_op jit(solution)/shard_map/jit(_take)/gather | solution.py:25
  195.6 33.5 %all-reduce.31.cloned.1.call-done = (f32[2560]{0:T(1024)}, f32[2560]{0:T(1024)}, f32[2560]{0:T(1024)}, f32[2560]{0:T(1024)}, f32[2560]{0:T(1024)}, /*index=5*/f32[2560]{0:T(1024)}, f32[2560]{0:T(1024)}) async-done(((f32[2560]{0:T(1024)}, f32[2560]{0:T(1024)}, f32[2560]{0:T(1024)}, f32[2560]{0:T(1024)}, f32[2560]{0:T(1024)}, /*index=5*/f32[2560]{0:T(1024)}, f32[2560]{0:T(1024)}), (f32[2560]{0:T(1024)}, ...) | async-done | bytes 71696 | tf_op jit(solution)/shard_map/psum | solution.py:29
  234.5 40.8 %all-reduce.32 = bf16[64,1024]{1,0:T(8,128)(2,1)S(1)} all-reduce(f32[64,1024]{1,0:T(8,128)S(1)} %fusion.94), channel_id=1, replica_groups=mesh['gene'=8,'cell'=4] {'gene'}, use_global_device_ids=true, to_apply=%region_2.4 | all-reduce | flops 65536 | bytes 393216 | tf_op jit(solution)/shard_map/psum | solution.py:34
  279.9 30.0 %all-reduce.17.cloned.1.call-done = bf16[64,2560]{1,0:T(8,128)(2,1)} async-done(((bf16[64,2560]{1,0:T(8,128)(2,1)}), bf16[64,2560]{1,0:T(8,128)(2,1)}) %all-reduce.17.cloned.1.call-update) | async-done | bytes 327696 | tf_op jit(solution)/shard_map/psum | solution.py:39
  311.8 30.9 %all-gather = f32[512,64]{1,0:T(8,128)S(1)} all-gather(f32[64,64]{1,0:T(8,128)S(1)} %fusion.116), channel_id=2, replica_groups=mesh['gene'=8,'cell'=4] {'gene'}, dimensions={0}, use_global_device_ids=true | all-gather | bytes 147456 | tf_op jit(solution)/shard_map/all_gather | solution.py:42
  361.3 40.1 %all-reduce.33 = bf16[64,1024]{1,0:T(8,128)(2,1)S(1)} all-reduce(f32[64,1024]{1,0:T(8,128)S(1)} %fusion.97), channel_id=1, replica_groups=mesh['gene'=8,'cell'=4] {'gene'}, use_global_device_ids=true, to_apply=%region_10.0 | all-reduce | flops 65536 | bytes 393216 | tf_op jit(solution)/shard_map/psum | solution.py:34
  406.0 29.0 %all-reduce.19.cloned.1.call-done = bf16[64,2560]{1,0:T(8,128)(2,1)} async-done(((bf16[64,2560]{1,0:T(8,128)(2,1)}), bf16[64,2560]{1,0:T(8,128)(2,1)}) %all-reduce.19.cloned.1.call-update) | async-done | bytes 327696 | tf_op jit(solution)/shard_map/psum | solution.py:39
  436.7 31.3 %all-gather.1 = f32[512,64]{1,0:T(8,128)S(1)} all-gather(f32[64,64]{1,0:T(8,128)S(1)} %fusion.118), channel_id=3, replica_groups=mesh['gene'=8,'cell'=4] {'gene'}, dimensions={0}, use_global_device_ids=true | all-gather | bytes 147456 | tf_op jit(solution)/shard_map/all_gather | solution.py:42
  486.7 40.2 %all-reduce.34 = bf16[64,1024]{1,0:T(8,128)(2,1)S(1)} all-reduce(f32[64,1024]{1,0:T(8,128)S(1)} %fusion.100), channel_id=1, replica_groups=mesh['gene'=8,'cell'=4] {'gene'}, use_global_device_ids=true, to_apply=%region_16.0 | all-reduce | flops 65536 | bytes 393216 | tf_op jit(solution)/shard_map/psum | solution.py:34
  531.5 29.0 %all-reduce.21.cloned.1.call-done = bf16[64,2560]{1,0:T(8,128)(2,1)} async-done(((bf16[64,2560]{1,0:T(8,128)(2,1)}), bf16[64,2560]{1,0:T(8,128)(2,1)}) %all-reduce.21.cloned.1.call-update) | async-done | bytes 327696 | tf_op jit(solution)/shard_map/psum | solution.py:39
  562.3 30.9 %all-gather.2 = f32[512,64]{1,0:T(8,128)S(1)} all-gather(f32[64,64]{1,0:T(8,128)S(1)} %fusion.120), channel_id=4, replica_groups=mesh['gene'=8,'cell'=4] {'gene'}, dimensions={0}, use_global_device_ids=true | all-gather | bytes 147456 | tf_op jit(solution)/shard_map/all_gather | solution.py:42
  611.8 40.1 %all-reduce.35 = bf16[64,1024]{1,0:T(8,128)(2,1)S(1)} all-reduce(f32[64,1024]{1,0:T(8,128)S(1)} %fusion.103), channel_id=1, replica_groups=mesh['gene'=8,'cell'=4] {'gene'}, use_global_device_ids=true, to_apply=%region_22.0 | all-reduce | flops 65536 | bytes 393216 | tf_op jit(solution)/shard_map/psum | solution.py:34
  656.7 28.8 %all-reduce.23.cloned.1.call-done = bf16[64,2560]{1,0:T(8,128)(2,1)} async-done(((bf16[64,2560]{1,0:T(8,128)(2,1)}), bf16[64,2560]{1,0:T(8,128)(2,1)}) %all-reduce.23.cloned.1.call-update) | async-done | bytes 327696 | tf_op jit(solution)/shard_map/psum | solution.py:39
  687.3 30.9 %all-gather.3 = f32[512,64]{1,0:T(8,128)S(1)} all-gather(f32[64,64]{1,0:T(8,128)S(1)} %fusion.122), channel_id=5, replica_groups=mesh['gene'=8,'cell'=4] {'gene'}, dimensions={0}, use_global_device_ids=true | all-gather | bytes 147456 | tf_op jit(solution)/shard_map/all_gather | solution.py:42
  736.8 40.1 %all-reduce.36 = bf16[64,1024]{1,0:T(8,128)(2,1)S(1)} all-reduce(f32[64,1024]{1,0:T(8,128)S(1)} %fusion.106), channel_id=1, replica_groups=mesh['gene'=8,'cell'=4] {'gene'}, use_global_device_ids=true, to_apply=%region_28.0 | all-reduce | flops 65536 | bytes 393216 | tf_op jit(solution)/shard_map/psum | solution.py:34
  781.5 29.0 %all-reduce.25.cloned.1.call-done = bf16[64,2560]{1,0:T(8,128)(2,1)} async-done(((bf16[64,2560]{1,0:T(8,128)(2,1)}), bf16[64,2560]{1,0:T(8,128)(2,1)}) %all-reduce.25.cloned.1.call-update) | async-done | bytes 327696 | tf_op jit(solution)/shard_map/psum | solution.py:39
  812.2 30.9 %all-gather.4 = f32[512,64]{1,0:T(8,128)S(1)} all-gather(f32[64,64]{1,0:T(8,128)S(1)} %fusion.124), channel_id=6, replica_groups=mesh['gene'=8,'cell'=4] {'gene'}, dimensions={0}, use_global_device_ids=true | all-gather | bytes 147456 | tf_op jit(solution)/shard_map/all_gather | solution.py:42
  861.8 40.3 %all-reduce.37 = bf16[64,1024]{1,0:T(8,128)(2,1)S(1)} all-reduce(f32[64,1024]{1,0:T(8,128)S(1)} %fusion.109), channel_id=1, replica_groups=mesh['gene'=8,'cell'=4] {'gene'}, use_global_device_ids=true, to_apply=%region_34.0 | all-reduce | flops 65536 | bytes 393216 | tf_op jit(solution)/shard_map/psum | solution.py:34
  906.7 29.0 %all-reduce.27.cloned.1.call-done = bf16[64,2560]{1,0:T(8,128)(2,1)} async-done(((bf16[64,2560]{1,0:T(8,128)(2,1)}), bf16[64,2560]{1,0:T(8,128)(2,1)}) %all-reduce.27.cloned.1.call-update) | async-done | bytes 327696 | tf_op jit(solution)/shard_map/psum | solution.py:39
  937.5 30.9 %all-gather.5 = f32[512,64]{1,0:T(8,128)S(1)} all-gather(f32[64,64]{1,0:T(8,128)S(1)} %fusion.126), channel_id=7, replica_groups=mesh['gene'=8,'cell'=4] {'gene'}, dimensions={0}, use_global_device_ids=true | all-gather | bytes 147456 | tf_op jit(solution)/shard_map/all_gather | solution.py:42
  987.0 40.0 %all-reduce.38 = bf16[64,1024]{1,0:T(8,128)(2,1)S(1)} all-reduce(f32[64,1024]{1,0:T(8,128)S(1)} %fusion.112), channel_id=1, replica_groups=mesh['gene'=8,'cell'=4] {'gene'}, use_global_device_ids=true, to_apply=%region_40.0 | all-reduce | flops 65536 | bytes 393216 | tf_op jit(solution)/shard_map/psum | solution.py:34
  1031.6 29.0 %all-reduce.29.cloned.1.call-done = bf16[64,2560]{1,0:T(8,128)(2,1)} async-done(((bf16[64,2560]{1,0:T(8,128)(2,1)}), bf16[64,2560]{1,0:T(8,128)(2,1)}) %all-reduce.29.cloned.1.call-update) | async-done | bytes 327696 | tf_op jit(solution)/shard_map/psum | solution.py:39
  1062.4 30.9 %all-gather.6 = f32[512,64]{1,0:T(8,128)S(1)} all-gather(f32[64,64]{1,0:T(8,128)S(1)} %fusion.127), channel_id=8, replica_groups=mesh['gene'=8,'cell'=4] {'gene'}, dimensions={0}, use_global_device_ids=true | all-gather | bytes 147456 | tf_op jit(solution)/shard_map/all_gather | solution.py:42
  (182 shorter events, 318.7 us)
Async XLA Ops:
  6.5 222.6 %all-reduce.31.cloned.1.call-start = ((), (), s32[]{:S(2)}) async-start(), calls=%async_computation.7 | async-start | bytes 172032 | tf_op jit(solution)/shard_map/psum | solution.py:29
  175.0 11.6 %slice-start = ((s8[5242880]{0:T(1024)(128)(4,1)}), s8[1048576]{0:T(1024)(128)(4,1)S(1)}, s32[]{:S(2)}) async-start(s8[5242880]{0:T(1024)(128)(4,1)} %bitcast.207), calls=%async_computation.8 | async-start | bytes 2097152
  179.3 7.3 slice-start.1
  179.3 12.7 %slice-start.2 = ((s8[5242880]{0:T(1024)(128)(4,1)}), s8[4194304]{0:T(1024)(128)(4,1)S(1)}, s32[]{:S(2)}) async-start(s8[5242880]{0:T(1024)(128)(4,1)} %bitcast.209), calls=%async_computation.10 | async-start | bytes 8388608
  179.3 12.7 %slice-start.4 = ((s8[5242880]{0:T(1024)(128)(4,1)}), s8[4194304]{0:T(1024)(128)(4,1)S(1)}, s32[]{:S(2)}) async-start(s8[5242880]{0:T(1024)(128)(4,1)} %bitcast.211), calls=%async_computation.12 | async-start | bytes 8388608
  186.6 5.4 slice-start.3
  186.6 5.4 slice-start.5
  192.0 37.8 %copy-start = (f32[64,2560]{1,0:T(8,128)S(1)}, f32[64,2560]{1,0:T(8,128)}, u32[]{:S(2)}) copy-start(f32[64,2560]{1,0:T(8,128)} %param.10) | copy-start | bytes 1966084
  195.6 114.4 %all-reduce.17.cloned.1.call-start = ((), (), s32[]{:S(2)}) async-start(), calls=%async_computation | async-start | bytes 655360 | tf_op jit(solution)/shard_map/psum | solution.py:39
  234.5 45.4 %copy-start.6 = (f32[2560]{0:T(1024)S(1)}, f32[2560]{0:T(1024)}, u32[]{:S(2)}) copy-start(f32[2560]{0:T(1024)} %get-tuple-element.8) | copy-start | bytes 30724
  279.8 155.1 %all-reduce.19.cloned.1.call-start = ((), (), s32[]{:S(2)}) async-start(), calls=%async_computation.1 | async-start | bytes 655360 | tf_op jit(solution)/shard_map/psum | solution.py:39
  361.3 44.7 %copy-start.5 = (f32[2560]{0:T(1024)S(1)}, f32[2560]{0:T(1024)}, u32[]{:S(2)}) copy-start(f32[2560]{0:T(1024)} %get-tuple-element.10) | copy-start | bytes 30724
  405.9 154.6 %all-reduce.21.cloned.1.call-start = ((), (), s32[]{:S(2)}) async-start(), calls=%async_computation.2 | async-start | bytes 655360 | tf_op jit(solution)/shard_map/psum | solution.py:39
  486.7 44.8 %copy-start.4 = (f32[2560]{0:T(1024)S(1)}, f32[2560]{0:T(1024)}, u32[]{:S(2)}) copy-start(f32[2560]{0:T(1024)} %get-tuple-element.11) | copy-start | bytes 30724
  531.4 154.0 %all-reduce.23.cloned.1.call-start = ((), (), s32[]{:S(2)}) async-start(), calls=%async_computation.3 | async-start | bytes 655360 | tf_op jit(solution)/shard_map/psum | solution.py:39
  611.8 44.8 %copy-start.3 = (f32[2560]{0:T(1024)S(1)}, f32[2560]{0:T(1024)}, u32[]{:S(2)}) copy-start(f32[2560]{0:T(1024)} %get-tuple-element.12) | copy-start | bytes 30724
  656.4 154.0 %all-reduce.25.cloned.1.call-start = ((), (), s32[]{:S(2)}) async-start(), calls=%async_computation.4 | async-start | bytes 655360 | tf_op jit(solution)/shard_map/psum | solution.py:39
  736.8 44.7 %copy-start.2 = (f32[2560]{0:T(1024)S(1)}, f32[2560]{0:T(1024)}, u32[]{:S(2)}) copy-start(f32[2560]{0:T(1024)} %get-tuple-element.13) | copy-start | bytes 30724
  781.4 154.2 %all-reduce.27.cloned.1.call-start = ((), (), s32[]{:S(2)}) async-start(), calls=%async_computation.5 | async-start | bytes 655360 | tf_op jit(solution)/shard_map/psum | solution.py:39
  861.8 44.9 %copy-start.1 = (f32[2560]{0:T(1024)S(1)}, f32[2560]{0:T(1024)}, u32[]{:S(2)}) copy-start(f32[2560]{0:T(1024)} %get-tuple-element.14) | copy-start | bytes 30724
  906.6 154.0 %all-reduce.29.cloned.1.call-start = ((), (), s32[]{:S(2)}) async-start(), calls=%async_computation.6 | async-start | bytes 655360 | tf_op jit(solution)/shard_map/psum | solution.py:39
Sparse Core Ops, SparseCore 0:
  195.7 33.3 all-reduce.30
  280.0 29.9 all-reduce.16
  406.0 28.8 all-reduce.18
  531.5 28.8 all-reduce.20
  656.5 28.8 all-reduce.22
  781.5 28.8 all-reduce.24
  906.7 28.8 all-reduce.26
  1031.7 28.8 all-reduce.28
